TPU v7x, 32 devices: a whole 2x2x4 slice. The times are simulated.
32 devices in a mesh: section: 16 (over z, y, core), tensor: 2 (over x).
Axes of the slice: x: 2, y: 2, z: 4, core: 2. Of those that a mesh axis runs over, the one named last changes fastest.
Arguments:
- saved: bfloat16 [16, 16, 64, 8192], P('section', None, 'tensor'), may hold values from -6 to 6
- offsets: int32 [16, 16], P('section'), may hold values from 0 to 15, as said below
Outputs:
- restored: float32 [16, 16, 64, 8192], P('section', None, None, 'tensor')
- block_sums: float32 [16, 16, 8192], P('section', None, 'tensor')
Inputs may be any that keep to these rules, and one draw needn't show every extreme that they name: Each row of offsets is a permutation of 0 to 15.
All inputs are finite; a program needn't handle non-finite values.
Results may differ from a plain program's by a relative error of at most 0.0003.
Values may be sent and summed in bfloat16 or wider, within the bound.
A program may use at most 128 MiB of HBM per device.

v0:
```python
import jax
import jax.numpy as jnp
from jax import lax
from jax.experimental import pallas as pl
from jax.experimental.pallas import tpu as pltpu
from jax.sharding import PartitionSpec as P

MESH = pl.DeviceIdType.MESH


def partner(index, step, count):
    if count & (count - 1):
        return (index + step) % count
    other = index
    bit = 1
    while bit < count:
        if step & bit:
            other = other + bit * (1 - 2 * ((index // bit) % 2))
        bit *= 2
    return other


def send_order(n, m):
    far = [(k, e) for k in range(n // 2, n) for e in range(m)]
    near = [(k, e) for k in range(n // 2 - 1, -1, -1) for e in range(m)]
    mixed = []
    for i in range(max(len(far), len(near))):
        mixed += far[i : i + 1] + near[i : i + 1]
    return mixed


def exchange(n, m, offsets, saved, arrived, held, out_box, load_sem, send_sem, recv_sem, own_sem):
    s = lax.axis_index("section")
    x = lax.axis_index("tensor")
    rows = saved.shape[1]
    cols = saved.shape[2] // m
    load = pltpu.make_async_copy(saved, held, load_sem)
    load.start()

    barrier = pltpu.get_barrier_semaphore()

    def greet(i, carry):
        j = i + 1
        pl.semaphore_signal(
            barrier,
            inc=1,
            device_id=((s + j // m) % n, (x + j % m) % m),
            device_id_type=MESH,
        )
        return carry

    lax.fori_loop(0, n * m - 1, greet, 0)
    load.wait()
    greeted = [False]

    def send(k, e):
        t = partner(s, k, n)
        d = partner(x, e, m)
        dst = arrived.at[s, pl.ds(x * rows, rows), :]
        if k == 0 and e == 0:
            return pltpu.make_async_copy(out_box.at[0], dst, own_sem)
        return pltpu.make_async_remote_copy(
            src_ref=out_box.at[k * m + e],
            dst_ref=dst,
            send_sem=send_sem.at[k * m + e],
            recv_sem=recv_sem.at[k * m + e],
            device_id=(t, d),
            device_id_type=MESH,
        )

    def fill(k, e):
        t = partner(s, k, n)
        d = partner(x, e, m)
        wanted = (t - s + n) % n
        slot = jnp.int32(0)
        for j in range(n):
            slot = jnp.where(offsets[0, j] == wanted, jnp.int32(j), slot)
        step = min(cols, 512)

        def move(i, carry):
            src = pl.ds(pl.multiple_of(d * cols + i * step, step), step)
            dst = pl.ds(pl.multiple_of(i * step, step), step)
            out_box[k * m + e, :, dst] = held[slot, :, src]
            return carry

        lax.fori_loop(0, cols // step, move, 0)

    copies = []
    waiting = None
    for k, e in send_order(n, m):
        fill(k, e)
        if waiting is not None:
            if not copies:
                pl.semaphore_wait(barrier, n * m - 1)
            copy = send(*waiting)
            copy.start()
            copies.append(copy)
        waiting = (k, e)
    copy = send(*waiting)
    copy.start()
    copies.append(copy)
    for copy in copies:
        copy.wait()


def widen(arrived, restored, sums, stage, stage_sem):
    blocks, rows, cols = arrived.shape
    depth = stage.shape[0]
    wide = min(cols, 512)
    copies = []
    for i in range(blocks):
        slot = i % depth
        if i >= depth:
            copies[i - depth].wait()
        for c in range(0, cols, wide):
            here = pl.ds(c, wide)
            total = None
            for r in range(0, rows, 16):
                band = pl.ds(r, min(16, rows - r))
                part = arrived[i, band, here].astype(jnp.float32)
                stage[slot, band, here] = part
                total = part if total is None else total + part
            sums[pl.ds(i, 1), here] = jnp.sum(total, axis=0, keepdims=True)
        copy = pltpu.make_async_copy(stage.at[slot], restored.at[i], stage_sem.at[slot])
        copy.start()
        copies.append(copy)
    for copy in copies[-depth:]:
        copy.wait()


def body(n, m, saved, offsets):
    _, slots, rows, width = saved.shape
    cols = width // m
    arrived = pl.pallas_call(
        lambda *refs: exchange(n, m, *refs),
        out_shape=jax.ShapeDtypeStruct((slots, rows * m, cols), saved.dtype),
        in_specs=[
            pl.BlockSpec(memory_space=pltpu.SMEM),
            pl.BlockSpec(memory_space=pltpu.HBM),
        ],
        out_specs=pl.BlockSpec(memory_space=pl.ANY),
        scratch_shapes=[
            pltpu.VMEM((slots, rows, width), saved.dtype),
            pltpu.VMEM((slots * m, rows, cols), saved.dtype),
            pltpu.SemaphoreType.DMA,
            pltpu.SemaphoreType.DMA((n * m,)),
            pltpu.SemaphoreType.DMA((n * m,)),
            pltpu.SemaphoreType.DMA,
        ],
        compiler_params=pltpu.CompilerParams(
            collective_id=0, has_side_effects=True, vmem_limit_bytes=20 * 2**20
        ),
        name="exchange",
    )(offsets, pltpu.with_memory_space_constraint(saved[0], pltpu.HBM))
    blocks, height = arrived.shape[:2]
    restored, block_sums = pl.pallas_call(
        widen,
        out_shape=[
            jax.ShapeDtypeStruct(arrived.shape, jnp.float32),
            jax.ShapeDtypeStruct((blocks, cols), jnp.float32),
        ],
        in_specs=[pl.BlockSpec(memory_space=pltpu.VMEM)],
        out_specs=[
            pl.BlockSpec(memory_space=pl.ANY),
            pl.BlockSpec(memory_space=pltpu.VMEM),
        ],
        scratch_shapes=[
            pltpu.VMEM((6, height, cols), jnp.float32),
            pltpu.SemaphoreType.DMA((6,)),
        ],
        compiler_params=pltpu.CompilerParams(vmem_limit_bytes=20 * 2**20),
        name="widen",
    )(arrived)
    return (restored[None], block_sums[None])


def solution(mesh):
    n = mesh.shape["section"]
    m = mesh.shape["tensor"]
    return jax.shard_map(
        lambda saved, offsets: body(n, m, saved, offsets),
        mesh=mesh,
        in_specs=(P("section", None, "tensor", None), P("section", None)),
        out_specs=(P("section", None, None, "tensor"), P("section", None, "tensor")),
        check_vma=False,
    )
```

profile of v0, /device:TPU:8, one launch (start us, length us, event | category | flops | bytes accessed | tf_op | source)
XLA Modules:
  0.0 196.1 jit_solution(2348803300956169513)
XLA Ops:
  0.6 0.0 copy-start
  0.6 0.6 copy-done
  1.3 188.1 %exchange.1.arrived = bf16[16,64,4096]{2,1,0:T(8,128)(2,1)S(1)} custom-call(s32[1,16]{1,0:T(1,128)S(1)} %copy-done, bf16[16,32,8192]{2,1,0:T(8,128)(2,1)} %bitcast.3), custom_call_target="tpu_custom_call" | custom-call | tf_op jit(solution)/shard_map/exchange/pallas_call | solution.py:134
  189.4 6.7 %widen.1 = (f32[16,64,4096]{2,1,0:T(8,128)}, f32[16,4096]{1,0:T(8,128)}) custom-call(bf16[16,64,4096]{2,1,0:T(8,128)(2,1)S(1)} %exchange.1.arrived), custom_call_target="tpu_custom_call" | custom-call | tf_op jit(solution)/shard_map/widen/pallas_call | solution.py:156
Async XLA Ops:
  0.6 0.7 copy-start
where the time goes:
time: 197 us; the launch traced here: 196 us
  Pallas kernels  195 us (99%)
    pallas_call x1, Pallas kernels, body(): pl.pallas_call(lambda *refs: exchange(n, m, *refs), out_shape=jax.ShapeDt...  188 us
    pallas_call x1, Pallas kernels, body(): pl.pallas_call(widen, out_shape=[jax.ShapeDtypeStruct(arrived.shape, jnp....  6.65 us

commit v1 on v0

v1 whole, which is shorter than its diff:
```python
import jax
import jax.numpy as jnp
from jax import lax
from jax.experimental import pallas as pl
from jax.experimental.pallas import tpu as pltpu
from jax.sharding import PartitionSpec as P

MESH = pl.DeviceIdType.MESH


def power_of_two(count):
    return count & (count - 1) == 0


def partner(index, step, count):
    if not power_of_two(count):
        return (index + step) % count
    other = index
    bit = 1
    while bit < count:
        if step & bit:
            other = other + bit * (1 - 2 * ((index // bit) % 2))
        bit *= 2
    return other


def late_steps(n):
    if n < 8 or not power_of_two(n):
        return []
    return list(range(3 * n // 4, n, 2))


def is_late(s, n):
    quarter = s // (n // 4)
    return ((quarter == 1) | (quarter == 2)) & (s % 2 == 0)


def send_order(n, m):
    late = late_steps(n)
    far_steps = [k for k in range(n // 2, n) if k not in late] + late
    far = [(k, e) for k in far_steps for e in range(m)]
    near = [(k, e) for k in range(n // 2 - 1, -1, -1) for e in range(m)]
    mixed = []
    for i in range(max(len(far), len(near))):
        mixed += far[i : i + 1] + near[i : i + 1]
    return mixed


def exchange(n, m, offsets, saved, arrived, kept, held, out_box, load_sem, send_sem, recv_sem, own_sem):
    s = lax.axis_index("section")
    x = lax.axis_index("tensor")
    rows = saved.shape[1]
    cols = saved.shape[2] // m
    late = late_steps(n)
    early = [k for k in range(n) if k not in late]
    load = pltpu.make_async_copy(saved, held, load_sem)
    load.start()

    barrier = pltpu.get_barrier_semaphore()

    def greet(i, carry):
        j = i + 1
        pl.semaphore_signal(
            barrier,
            inc=1,
            device_id=((s + j // m) % n, (x + j % m) % m),
            device_id_type=MESH,
        )
        return carry

    lax.fori_loop(0, n * m - 1, greet, 0)
    load.wait()

    def box(k, e):
        if k in late:
            return kept.at[late.index(k) * m + e]
        return out_box.at[early.index(k) * m + e]

    def send(k, e):
        t = partner(s, k, n)
        d = partner(x, e, m)
        dst = arrived.at[s, pl.ds(x * rows, rows), :]
        if k == 0 and e == 0:
            return pltpu.make_async_copy(box(k, e), dst, own_sem)
        return pltpu.make_async_remote_copy(
            src_ref=box(k, e),
            dst_ref=dst,
            send_sem=send_sem.at[k * m + e],
            recv_sem=recv_sem.at[k * m + e],
            device_id=(t, d),
            device_id_type=MESH,
        )

    def fill(k, e):
        t = partner(s, k, n)
        d = partner(x, e, m)
        wanted = (t - s + n) % n
        slot = jnp.int32(0)
        for j in range(n):
            slot = jnp.where(offsets[0, j] == wanted, jnp.int32(j), slot)
        step = min(cols, 512)
        to = box(k, e)

        def move(i, carry):
            src = pl.ds(pl.multiple_of(d * cols + i * step, step), step)
            dst = pl.ds(pl.multiple_of(i * step, step), step)
            to[:, dst] = held[slot, :, src]
            return carry

        lax.fori_loop(0, cols // step, move, 0)

    def start(k, e):
        copy = send(k, e)
        if k in late:
            pl.when(jnp.logical_not(is_late(s, n)))(copy.start)
        else:
            copy.start()
        copies.append((k, copy))

    copies = []
    waiting = None
    for k, e in send_order(n, m):
        fill(k, e)
        if waiting is not None:
            if not copies:
                pl.semaphore_wait(barrier, n * m - 1)
            start(*waiting)
        waiting = (k, e)
    start(*waiting)
    for k, copy in copies:
        if k not in late:
            copy.wait()

    if late:

        @pl.when(jnp.logical_not(is_late(s, n)))
        def _():
            for k, copy in copies:
                if k in late:
                    copy.wait()


def exchange_late(n, m, kept, sums, arrived, send_sem, recv_sem):
    s = lax.axis_index("section")
    x = lax.axis_index("tensor")
    rows = kept.shape[1]
    late = late_steps(n)
    pairs = [(k, e) for k in late for e in range(m)]
    barrier = pltpu.get_barrier_semaphore()

    @pl.when(is_late(s, n))
    def _():
        for k, e in pairs:
            pl.semaphore_signal(
                barrier,
                inc=1,
                device_id=(partner(s, k, n), partner(x, e, m)),
                device_id_type=MESH,
            )
        pl.semaphore_wait(barrier, len(pairs))
        copies = []
        for i, (k, e) in enumerate(pairs):
            copy = pltpu.make_async_remote_copy(
                src_ref=kept.at[i],
                dst_ref=arrived.at[late.index(k), pl.ds(x * rows, rows), :],
                send_sem=send_sem.at[i],
                recv_sem=recv_sem.at[i],
                device_id=(partner(s, k, n), partner(x, e, m)),
                device_id_type=MESH,
            )
            copy.start()
            copies.append(copy)
        for copy in copies:
            copy.wait()


def widen_block(arrived, i, restored, sums, at, stage, sem):
    _, rows, cols = arrived.shape
    wide = min(cols, 512)
    for c in range(0, cols, wide):
        here = pl.ds(c, wide)
        total = None
        for r in range(0, rows, 16):
            band = pl.ds(r, min(16, rows - r))
            part = arrived[i, band, here].astype(jnp.float32)
            stage[band, here] = part
            total = part if total is None else total + part
        sums[pl.ds(at, 1), here] = jnp.sum(total, axis=0, keepdims=True)
    copy = pltpu.make_async_copy(stage, restored.at[at], sem)
    copy.start()
    return copy


def widen(n, arrived, restored, sums, stage, table, stage_sem):
    s = lax.axis_index("section")
    late = late_steps(n)
    depth = stage.shape[0] - len(late)
    copies = []
    for k in range(n):
        if k in late:
            continue
        slot = len(copies) % depth
        if len(copies) >= depth:
            copies[len(copies) - depth].wait()
        i = partner(s, k, n)
        copies.append(
            widen_block(arrived, i, restored, table, i, stage.at[slot], stage_sem.at[slot])
        )
    if late:

        @pl.when(jnp.logical_not(is_late(s, n)))
        def _():
            rest = []
            for j, k in enumerate(late):
                i = partner(s, k, n)
                slot = depth + j
                rest.append(
                    widen_block(arrived, i, restored, table, i, stage.at[slot], stage_sem.at[slot])
                )
            for copy in rest:
                copy.wait()

    sums[...] = table[pl.ds(0, n), :]
    for copy in copies[-depth:]:
        copy.wait()


def widen_late(n, arrived, given, sums, restored, sums_out, stage, table, stage_sem, table_sem):
    s = lax.axis_index("section")
    late = late_steps(n)
    table[pl.ds(0, n), :] = sums[...]

    @pl.when(is_late(s, n))
    def _():
        rest = []
        for j, k in enumerate(late):
            i = partner(s, k, n)
            rest.append(
                widen_block(arrived, j, restored, table, i, stage.at[j], stage_sem.at[j])
            )
        for copy in rest:
            copy.wait()

    copy = pltpu.make_async_copy(table.at[pl.ds(0, n), :], sums_out, table_sem)
    copy.start()
    copy.wait()


def body(n, m, saved, offsets):
    _, slots, rows, width = saved.shape
    cols = width // m
    late = len(late_steps(n))
    arrived, kept = pl.pallas_call(
        lambda *refs: exchange(n, m, *refs),
        out_shape=[
            jax.ShapeDtypeStruct((slots, rows * m, cols), saved.dtype),
            jax.ShapeDtypeStruct((max(late * m, 1), rows, cols), saved.dtype),
        ],
        in_specs=[
            pl.BlockSpec(memory_space=pltpu.SMEM),
            pl.BlockSpec(memory_space=pltpu.HBM),
        ],
        out_specs=[
            pl.BlockSpec(memory_space=pl.ANY),
            pl.BlockSpec(memory_space=pltpu.VMEM),
        ],
        scratch_shapes=[
            pltpu.VMEM((slots, rows, width), saved.dtype),
            pltpu.VMEM(((slots - late) * m, rows, cols), saved.dtype),
            pltpu.SemaphoreType.DMA,
            pltpu.SemaphoreType.DMA((n * m,)),
            pltpu.SemaphoreType.DMA((n * m,)),
            pltpu.SemaphoreType.DMA,
        ],
        compiler_params=pltpu.CompilerParams(
            collective_id=0, has_side_effects=True, vmem_limit_bytes=20 * 2**20
        ),
        name="exchange",
    )(offsets, pltpu.with_memory_space_constraint(saved[0], pltpu.HBM))
    blocks, height = arrived.shape[:2]
    restored, block_sums = pl.pallas_call(
        lambda *refs: widen(n, *refs),
        out_shape=[
            jax.ShapeDtypeStruct(arrived.shape, jnp.float32),
            jax.ShapeDtypeStruct((blocks, cols), jnp.float32),
        ],
        in_specs=[pl.BlockSpec(memory_space=pltpu.VMEM)],
        out_specs=[
            pl.BlockSpec(memory_space=pl.ANY),
            pl.BlockSpec(memory_space=pltpu.VMEM),
        ],
        scratch_shapes=[
            pltpu.VMEM((6 + late, height, cols), jnp.float32),
            pltpu.VMEM((blocks + 8, cols), jnp.float32),
            pltpu.SemaphoreType.DMA((6 + late,)),
        ],
        compiler_params=pltpu.CompilerParams(vmem_limit_bytes=20 * 2**20),
        name="widen",
    )(arrived)
    if late:
        arrived = pl.pallas_call(
            lambda *refs: exchange_late(n, m, *refs),
            out_shape=jax.ShapeDtypeStruct((late, rows * m, cols), saved.dtype),
            in_specs=[
                pl.BlockSpec(memory_space=pltpu.VMEM),
                pl.BlockSpec(memory_space=pl.ANY),
            ],
            out_specs=pl.BlockSpec(memory_space=pl.ANY),
            scratch_shapes=[
                pltpu.SemaphoreType.DMA((late * m,)),
                pltpu.SemaphoreType.DMA((late * m,)),
            ],
            compiler_params=pltpu.CompilerParams(
                collective_id=1, has_side_effects=True, vmem_limit_bytes=8 * 2**20
            ),
            name="exchange_late",
        )(kept, block_sums)
        restored, block_sums = pl.pallas_call(
            lambda *refs: widen_late(n, *refs),
            out_shape=[
                jax.ShapeDtypeStruct(restored.shape, jnp.float32),
                jax.ShapeDtypeStruct(block_sums.shape, jnp.float32),
            ],
            in_specs=[
                pl.BlockSpec(memory_space=pltpu.VMEM),
                pl.BlockSpec(memory_space=pl.ANY),
                pl.BlockSpec(memory_space=pltpu.VMEM),
            ],
            out_specs=[
                pl.BlockSpec(memory_space=pl.ANY),
                pl.BlockSpec(memory_space=pl.ANY),
            ],
            scratch_shapes=[
                pltpu.VMEM((late, height, cols), jnp.float32),
                pltpu.VMEM((blocks + 8, cols), jnp.float32),
                pltpu.SemaphoreType.DMA((late,)),
                pltpu.SemaphoreType.DMA,
            ],
            input_output_aliases={1: 0},
            compiler_params=pltpu.CompilerParams(vmem_limit_bytes=20 * 2**20),
            name="widen_late",
        )(arrived, restored, block_sums)
    return (restored[None], block_sums[None])


def solution(mesh):
    n = mesh.shape["section"]
    m = mesh.shape["tensor"]
    return jax.shard_map(
        lambda saved, offsets: body(n, m, saved, offsets),
        mesh=mesh,
        in_specs=(P("section", None, "tensor", None), P("section", None)),
        out_specs=(P("section", None, None, "tensor"), P("section", None, "tensor")),
        check_vma=False,
    )
```

time: 197 us -> 192 us (0.975)
  Pallas kernels: 195 us -> 191 us
    pallas_call x2 -> x4, Pallas kernels: 195 us -> 191 us  [the longest x1 166 us: body(): pl.pallas_call(lambda *refs: exchange(n, m, *refs), out_shape=[jax.ShapeD...]
where the time goes in v1:
time: 192 us
  Pallas kernels  191 us (99%)
    pallas_call x1, Pallas kernels, body(): pl.pallas_call(lambda *refs: exchange(n, m, *refs), out_shape=[jax.ShapeD...  166 us
    pallas_call x1, Pallas kernels, body(): pl.pallas_call(lambda *refs: exchange_late(n, m, *refs), out_shape=jax.Sh...  17.4 us
    pallas_call x1, Pallas kernels, body(): pl.pallas_call(lambda *refs: widen(n, *refs), out_shape=[jax.ShapeDtypeSt...  5.35 us

profile of v1, /device:TPU:8, one launch (start us, length us, event | category | flops | bytes accessed | tf_op | source)
XLA Modules:
  0.0 191.8 jit_solution(17305327211271535483)
XLA Ops:
  0.6 0.0 copy-start
  0.6 0.6 copy-done
  1.3 165.6 %exchange.1 = (bf16[16,64,4096]{2,1,0:T(8,128)(2,1)S(1)}, bf16[4,32,4096]{2,1,0:T(8,128)(2,1)S(1)}) custom-call(s32[1,16]{1,0:T(1,128)S(1)} %copy-done, bf16[16,32,8192]{2,1,0:T(8,128)(2,1)} %bitcast.4), custom_call_target="tpu_custom_call" | custom-call | tf_op jit(solution)/shard_map/exchange/pallas_call | solution.py:253
  166.9 5.4 %widen.1 = (f32[16,64,4096]{2,1,0:T(8,128)}, f32[16,4096]{1,0:T(8,128)S(1)}) custom-call(bf16[16,64,4096]{2,1,0:T(8,128)(2,1)S(1)} %get-tuple-element.9.refs_0_), custom_call_target="tpu_custom_call" | custom-call | tf_op jit(solution)/shard_map/widen/pallas_call | solution.py:281
  172.3 17.4 %exchange_late.1.refs_0_ = bf16[2,64,4096]{2,1,0:T(8,128)(2,1)S(1)} custom-call(bf16[4,32,4096]{2,1,0:T(8,128)(2,1)S(1)} %get-tuple-element.8.refs_0_, f32[16,4096]{1,0:T(8,128)S(1)} %get-tuple-element.10.refs_1_.refs_2_), custom_call_target="tpu_custom_call" | custom-call | tf_op jit(solution)/shard_map/exchange_late/pallas_call | solution.py:301
  189.7 2.2 %widen_late.1 = (f32[16,64,4096]{2,1,0:T(8,128)}, f32[16,4096]{1,0:T(8,128)}) custom-call(bf16[2,64,4096]{2,1,0:T(8,128)(2,1)S(1)} %exchange_late.1.refs_0_, f32[16,64,4096]{2,1,0:T(8,128)} %get-tuple-element.11.refs_1_, f32[16,4096]{1,0:T(8,128)S(1)} %get-tuple-element.10.refs_1_.refs_2_), custom_call_target="tpu_custom_call", output_to_operand_aliasing={{0}: (1, {})} | custom-call | tf_op jit(solution)/shard_map/widen_late/pallas_call | solution.py:318
Async XLA Ops:
  0.6 0.7 copy-start

commit v2 on v1

--- a/solution.py
+++ b/solution.py
@@ -30,9 +30,17 @@
     return list(range(3 * n // 4, n, 2))
 
 
+def is_inner(s, n):
+    quarter = s // (n // 4)
+    return (quarter == 1) | (quarter == 2)
+
+
 def is_late(s, n):
-    quarter = s // (n // 4)
-    return ((quarter == 1) | (quarter == 2)) & (s % 2 == 0)
+    return is_inner(s, n) & (s % 2 == 0)
+
+
+def early_step(n):
+    return 3 * n // 4 + 1
 
 
 def send_order(n, m):
@@ -46,39 +54,113 @@
     return mixed
 
 
-def exchange(n, m, offsets, saved, arrived, kept, held, out_box, load_sem, send_sem, recv_sem, own_sem):
+def parts_of(rows):
+    return 2 if rows % 32 == 0 else 1
+
+
+def signal(barrier, t, d):
+    pl.semaphore_signal(barrier, inc=1, device_id=(t, d), device_id_type=MESH)
+
+
+def greet_outer(barrier, n, m, first, s, x):
+    half = n // 2
+
+    def greet(j, carry):
+        place = (s + j // m) % half
+        t = jnp.where(place < n // 4, place, place + half)
+        signal(barrier, t, (x + j % m) % m)
+        return carry
+
+    lax.fori_loop(first, half * m, greet, 0)
+
+
+def greet_all(barrier, n, m, s, x):
+    def greet(j, carry):
+        signal(barrier, (s + j // m) % n, (x + j % m) % m)
+        return carry
+
+    lax.fori_loop(1, n * m, greet, 0)
+
+
+def exchange(
+    n, m, offsets, saved, arrived, kept, table, rest, out_box,
+    table_sem, load_sem, send_sem, recv_sem, own_sem, part_sem, *pieces,
+):
     s = lax.axis_index("section")
     x = lax.axis_index("tensor")
     rows = saved.shape[1]
     cols = saved.shape[2] // m
+    parts = len(pieces)
+    part = rows // parts
     late = late_steps(n)
+    staged = bool(late)
+    first = early_step(n) if staged else n // 2
+    barrier = pltpu.get_barrier_semaphore()
+    inner = is_inner(s, n) if staged else None
+
+    tabled = pltpu.make_async_copy(offsets, table, table_sem)
+    tabled.start()
+    own = pl.ds(pl.multiple_of(x * cols, cols), cols)
+    loads = [
+        pltpu.make_async_copy(saved.at[:, pl.ds(h * part, part), own], piece, load_sem.at[h])
+        for h, piece in enumerate(pieces)
+    ]
+    for e in range(1, m):
+        d = partner(x, e, m)
+        those = pl.ds(pl.multiple_of(d * cols, cols), cols)
+        loads.append(
+            pltpu.make_async_copy(saved.at[:, :, those], rest.at[e - 1], load_sem.at[parts - 1 + e])
+        )
+    for load in loads:
+        load.start()
+
+    if staged:
+
+        @pl.when(inner)
+        def _():
+            signal(barrier, partner(s, first, n), x)
+
+        @pl.when(jnp.logical_not(inner))
+        def _():
+            greet_outer(barrier, n, m, 1, jnp.where(s < n // 4, s, s - n // 2), x)
+
+    else:
+        greet_all(barrier, n, m, s, x)
+
     early = [k for k in range(n) if k not in late]
-    load = pltpu.make_async_copy(saved, held, load_sem)
-    load.start()
-
-    barrier = pltpu.get_barrier_semaphore()
-
-    def greet(i, carry):
-        j = i + 1
-        pl.semaphore_signal(
-            barrier,
-            inc=1,
-            device_id=((s + j // m) % n, (x + j % m) % m),
-            device_id_type=MESH,
-        )
-        return carry
-
-    lax.fori_loop(0, n * m - 1, greet, 0)
-    load.wait()
 
     def box(k, e):
         if k in late:
             return kept.at[late.index(k) * m + e]
         return out_box.at[early.index(k) * m + e]
 
+    def slot_of(k):
+        wanted = (partner(s, k, n) - s + n) % n
+        slot = jnp.int32(0)
+        for j in range(n):
+            slot = jnp.where(table[0, j] == wanted, jnp.int32(j), slot)
+        return slot
+
+    def fill(held, slot, to):
+        step = min(cols, 512)
+
+        def move(i, carry):
+            here = pl.ds(pl.multiple_of(i * step, step), step)
+            to[:, here] = held[slot, :, here]
+            return carry
+
+        lax.fori_loop(0, cols // step, move, 0)
+
+    def fill_block(k, e):
+        slot = slot_of(k)
+        to = box(k, e)
+        if e == 0:
+            for h, piece in enumerate(pieces):
+                fill(piece, slot, to.at[pl.ds(h * part, part), :])
+        else:
+            fill(rest.at[e - 1], slot, to)
+
     def send(k, e):
-        t = partner(s, k, n)
-        d = partner(x, e, m)
         dst = arrived.at[s, pl.ds(x * rows, rows), :]
         if k == 0 and e == 0:
             return pltpu.make_async_copy(box(k, e), dst, own_sem)
@@ -87,27 +169,47 @@
             dst_ref=dst,
             send_sem=send_sem.at[k * m + e],
             recv_sem=recv_sem.at[k * m + e],
-            device_id=(t, d),
+            device_id=(partner(s, k, n), partner(x, e, m)),
             device_id_type=MESH,
         )
 
-    def fill(k, e):
-        t = partner(s, k, n)
-        d = partner(x, e, m)
-        wanted = (t - s + n) % n
-        slot = jnp.int32(0)
-        for j in range(n):
-            slot = jnp.where(offsets[0, j] == wanted, jnp.int32(j), slot)
-        step = min(cols, 512)
-        to = box(k, e)
-
-        def move(i, carry):
-            src = pl.ds(pl.multiple_of(d * cols + i * step, step), step)
-            dst = pl.ds(pl.multiple_of(i * step, step), step)
-            to[:, dst] = held[slot, :, src]
-            return carry
-
-        lax.fori_loop(0, cols // step, move, 0)
+    def send_part(h):
+        return pltpu.make_async_remote_copy(
+            src_ref=box(first, 0).at[pl.ds(h * part, part), :],
+            dst_ref=arrived.at[s, pl.ds(x * rows + h * part, part), :],
+            send_sem=part_sem.at[h],
+            recv_sem=part_sem.at[parts + h],
+            device_id=(partner(s, first, n), x),
+            device_id_type=MESH,
+        )
+
+    firsts = [send_part(h) for h in range(parts)]
+    tabled.wait()
+    slot = slot_of(first)
+    for h in range(parts):
+        loads[h].wait()
+        fill(pieces[h], slot, box(first, 0).at[pl.ds(h * part, part), :])
+        if h > 0:
+            firsts[h].start()
+        elif staged:
+
+            @pl.when(inner)
+            def _():
+                pl.semaphore_wait(barrier, 1)
+                firsts[0].start()
+                greet_outer(barrier, n, m, 0, 0, 0)
+
+            @pl.when(jnp.logical_not(inner))
+            def _():
+                pl.semaphore_wait(barrier, n * m - 1)
+                signal(barrier, partner(s, n // 4, n), x)
+                firsts[0].start()
+
+        else:
+            pl.semaphore_wait(barrier, n * m - 1)
+            firsts[0].start()
+    for load in loads[parts:]:
+        load.wait()
 
     def start(k, e):
         copy = send(k, e)
@@ -120,13 +222,21 @@
     copies = []
     waiting = None
     for k, e in send_order(n, m):
-        fill(k, e)
+        if k == first and e == 0:
+            continue
+        fill_block(k, e)
         if waiting is not None:
-            if not copies:
-                pl.semaphore_wait(barrier, n * m - 1)
+            if staged and not copies:
+
+                @pl.when(inner)
+                def _():
+                    pl.semaphore_wait(barrier, 1)
+
             start(*waiting)
         waiting = (k, e)
     start(*waiting)
+    for copy in firsts:
+        copy.wait()
     for k, copy in copies:
         if k not in late:
             copy.wait()
@@ -250,6 +360,7 @@
     _, slots, rows, width = saved.shape
     cols = width // m
     late = len(late_steps(n))
+    parts = parts_of(rows)
     arrived, kept = pl.pallas_call(
         lambda *refs: exchange(n, m, *refs),
         out_shape=[
@@ -257,7 +368,7 @@
             jax.ShapeDtypeStruct((max(late * m, 1), rows, cols), saved.dtype),
         ],
         in_specs=[
-            pl.BlockSpec(memory_space=pltpu.SMEM),
+            pl.BlockSpec(memory_space=pltpu.HBM),
             pl.BlockSpec(memory_space=pltpu.HBM),
         ],
         out_specs=[
@@ -265,18 +376,25 @@
             pl.BlockSpec(memory_space=pltpu.VMEM),
         ],
         scratch_shapes=[
-            pltpu.VMEM((slots, rows, width), saved.dtype),
+            pltpu.SMEM(offsets.shape, offsets.dtype),
+            pltpu.VMEM((max(m - 1, 1), slots, rows, cols), saved.dtype),
             pltpu.VMEM(((slots - late) * m, rows, cols), saved.dtype),
             pltpu.SemaphoreType.DMA,
+            pltpu.SemaphoreType.DMA((parts + m - 1,)),
             pltpu.SemaphoreType.DMA((n * m,)),
             pltpu.SemaphoreType.DMA((n * m,)),
             pltpu.SemaphoreType.DMA,
-        ],
+            pltpu.SemaphoreType.DMA((2 * parts,)),
+        ]
+        + [pltpu.VMEM((slots, rows // parts, cols), saved.dtype)] * parts,
         compiler_params=pltpu.CompilerParams(
             collective_id=0, has_side_effects=True, vmem_limit_bytes=20 * 2**20
         ),
         name="exchange",
-    )(offsets, pltpu.with_memory_space_constraint(saved[0], pltpu.HBM))
+    )(
+        pltpu.with_memory_space_constraint(offsets, pltpu.HBM),
+        pltpu.with_memory_space_constraint(saved[0], pltpu.HBM),
+    )
     blocks, height = arrived.shape[:2]
     restored, block_sums = pl.pallas_call(
         lambda *refs: widen(n, *refs),

time: 192 us -> 189 us (0.984)
  Pallas kernels: 191 us -> 188 us
    pallas_call x1, Pallas kernels: 166 us -> 163 us  [body(): pl.pallas_call(lambda *refs: exchange(n, m, *refs), out_shape=[jax.ShapeD...]
where the time goes in v2:
time: 189 us
  Pallas kernels  188 us (99%)
    pallas_call x1, Pallas kernels, body(): pl.pallas_call(lambda *refs: exchange(n, m, *refs), out_shape=[jax.ShapeD...  163 us
    pallas_call x1, Pallas kernels, body(): pl.pallas_call(lambda *refs: exchange_late(n, m, *refs), out_shape=jax.Sh...  17.4 us
    pallas_call x1, Pallas kernels, body(): pl.pallas_call(lambda *refs: widen(n, *refs), out_shape=[jax.ShapeDtypeSt...  5.35 us

profile of v2, /device:TPU:8, one launch (start us, length us, event | category | flops | bytes accessed | tf_op | source)
XLA Modules:
  0.0 188.7 jit_solution(3722639732641823705)
XLA Ops:
  0.6 163.2 %exchange.1 = (bf16[16,64,4096]{2,1,0:T(8,128)(2,1)S(1)}, bf16[4,32,4096]{2,1,0:T(8,128)(2,1)S(1)}) custom-call(s32[1,16]{1,0:T(1,128)} %refs_0_.1, bf16[16,32,8192]{2,1,0:T(8,128)(2,1)} %bitcast.4), custom_call_target="tpu_custom_call" | custom-call | tf_op jit(solution)/shard_map/exchange/pallas_call | solution.py:364
  163.8 5.4 %widen.1 = (f32[16,64,4096]{2,1,0:T(8,128)}, f32[16,4096]{1,0:T(8,128)S(1)}) custom-call(bf16[16,64,4096]{2,1,0:T(8,128)(2,1)S(1)} %get-tuple-element.9.refs_0_), custom_call_target="tpu_custom_call" | custom-call | tf_op jit(solution)/shard_map/widen/pallas_call | solution.py:399
  169.2 17.4 %exchange_late.1.refs_0_ = bf16[2,64,4096]{2,1,0:T(8,128)(2,1)S(1)} custom-call(bf16[4,32,4096]{2,1,0:T(8,128)(2,1)S(1)} %get-tuple-element.8.refs_0_, f32[16,4096]{1,0:T(8,128)S(1)} %get-tuple-element.10.refs_1_.refs_2_), custom_call_target="tpu_custom_call" | custom-call | tf_op jit(solution)/shard_map/exchange_late/pallas_call | solution.py:419
  186.5 2.2 %widen_late.1 = (f32[16,64,4096]{2,1,0:T(8,128)}, f32[16,4096]{1,0:T(8,128)}) custom-call(bf16[2,64,4096]{2,1,0:T(8,128)(2,1)S(1)} %exchange_late.1.refs_0_, f32[16,64,4096]{2,1,0:T(8,128)} %get-tuple-element.11.refs_1_, f32[16,4096]{1,0:T(8,128)S(1)} %get-tuple-element.10.refs_1_.refs_2_), custom_call_target="tpu_custom_call", output_to_operand_aliasing={{0}: (1, {})} | custom-call | tf_op jit(solution)/shard_map/widen_late/pallas_call | solution.py:436

commit v3 on v2

--- a/solution.py
+++ b/solution.py
@@ -36,7 +36,7 @@
 
 
 def is_late(s, n):
-    return is_inner(s, n) & (s % 2 == 0)
+    return is_inner(s, n) & (s % 2 == 1)
 
 
 def early_step(n):
@@ -54,8 +54,10 @@
     return mixed
 
 
-def parts_of(rows):
-    return 2 if rows % 32 == 0 else 1
+def parts_of(cols):
+    if cols % 1024:
+        return [cols]
+    return [cols // 8, cols // 8, cols // 4, cols // 2]
 
 
 def signal(barrier, t, d):
@@ -91,7 +93,8 @@
     rows = saved.shape[1]
     cols = saved.shape[2] // m
     parts = len(pieces)
-    part = rows // parts
+    widths = parts_of(cols)
+    starts = [sum(widths[:h]) for h in range(parts)]
     late = late_steps(n)
     staged = bool(late)
     first = early_step(n) if staged else n // 2
@@ -100,11 +103,10 @@
 
     tabled = pltpu.make_async_copy(offsets, table, table_sem)
     tabled.start()
-    own = pl.ds(pl.multiple_of(x * cols, cols), cols)
-    loads = [
-        pltpu.make_async_copy(saved.at[:, pl.ds(h * part, part), own], piece, load_sem.at[h])
-        for h, piece in enumerate(pieces)
-    ]
+    loads = []
+    for h, piece in enumerate(pieces):
+        own = pl.ds(pl.multiple_of(x * cols + starts[h], widths[0]), widths[h])
+        loads.append(pltpu.make_async_copy(saved.at[:, :, own], piece, load_sem.at[h]))
     for e in range(1, m):
         d = partner(x, e, m)
         those = pl.ds(pl.multiple_of(d * cols, cols), cols)
@@ -141,22 +143,24 @@
             slot = jnp.where(table[0, j] == wanted, jnp.int32(j), slot)
         return slot
 
-    def fill(held, slot, to):
-        step = min(cols, 512)
+    def fill(held, slot, to, at=0):
+        width = held.shape[-1]
+        step = min(width, 512)
 
         def move(i, carry):
             here = pl.ds(pl.multiple_of(i * step, step), step)
-            to[:, here] = held[slot, :, here]
+            there = pl.ds(pl.multiple_of(at + i * step, widths[0]), step)
+            to[:, there] = held[slot, :, here]
             return carry
 
-        lax.fori_loop(0, cols // step, move, 0)
+        lax.fori_loop(0, width // step, move, 0)
 
     def fill_block(k, e):
         slot = slot_of(k)
         to = box(k, e)
         if e == 0:
             for h, piece in enumerate(pieces):
-                fill(piece, slot, to.at[pl.ds(h * part, part), :])
+                fill(piece, slot, to, starts[h])
         else:
             fill(rest.at[e - 1], slot, to)
 
@@ -175,8 +179,8 @@
 
     def send_part(h):
         return pltpu.make_async_remote_copy(
-            src_ref=box(first, 0).at[pl.ds(h * part, part), :],
-            dst_ref=arrived.at[s, pl.ds(x * rows + h * part, part), :],
+            src_ref=box(first, 0).at[:, pl.ds(starts[h], widths[h])],
+            dst_ref=arrived.at[s, pl.ds(x * rows, rows), pl.ds(starts[h], widths[h])],
             send_sem=part_sem.at[h],
             recv_sem=part_sem.at[parts + h],
             device_id=(partner(s, first, n), x),
@@ -184,20 +188,25 @@
         )
 
     firsts = [send_part(h) for h in range(parts)]
+    if staged:
+
+        @pl.when(inner)
+        def _():
+            pl.semaphore_wait(barrier, 1)
+            greet_outer(barrier, n, m, 0, 0, 0)
+
     tabled.wait()
     slot = slot_of(first)
     for h in range(parts):
         loads[h].wait()
-        fill(pieces[h], slot, box(first, 0).at[pl.ds(h * part, part), :])
+        fill(pieces[h], slot, box(first, 0), starts[h])
         if h > 0:
             firsts[h].start()
         elif staged:
 
             @pl.when(inner)
             def _():
-                pl.semaphore_wait(barrier, 1)
                 firsts[0].start()
-                greet_outer(barrier, n, m, 0, 0, 0)
 
             @pl.when(jnp.logical_not(inner))
             def _():
@@ -269,7 +278,7 @@
             )
         pl.semaphore_wait(barrier, len(pairs))
         copies = []
-        for i, (k, e) in enumerate(pairs):
+        for i, (k, e) in reversed(list(enumerate(pairs))):
             copy = pltpu.make_async_remote_copy(
                 src_ref=kept.at[i],
                 dst_ref=arrived.at[late.index(k), pl.ds(x * rows, rows), :],
@@ -284,7 +293,7 @@
             copy.wait()
 
 
-def widen_block(arrived, i, restored, sums, at, stage, sem):
+def widen_block(arrived, i, restored, sums, at, stage, sem, eager=False):
     _, rows, cols = arrived.shape
     wide = min(cols, 512)
     for c in range(0, cols, wide):
@@ -296,6 +305,10 @@
             stage[band, here] = part
             total = part if total is None else total + part
         sums[pl.ds(at, 1), here] = jnp.sum(total, axis=0, keepdims=True)
+        if eager:
+            pltpu.make_async_copy(stage.at[:, here], restored.at[at, :, here], sem).start()
+    if eager:
+        return None
     copy = pltpu.make_async_copy(stage, restored.at[at], sem)
     copy.start()
     return copy
@@ -340,19 +353,23 @@
     late = late_steps(n)
     table[pl.ds(0, n), :] = sums[...]
 
+    places = [partner(s, k, n) for k in late]
+
     @pl.when(is_late(s, n))
     def _():
-        rest = []
-        for j, k in enumerate(late):
-            i = partner(s, k, n)
-            rest.append(
-                widen_block(arrived, j, restored, table, i, stage.at[j], stage_sem.at[j])
+        for j, i in enumerate(places):
+            widen_block(
+                arrived, j, restored, table, i, stage.at[j], stage_sem.at[j], eager=True
             )
-        for copy in rest:
-            copy.wait()
 
     copy = pltpu.make_async_copy(table.at[pl.ds(0, n), :], sums_out, table_sem)
     copy.start()
+
+    @pl.when(is_late(s, n))
+    def _():
+        for j, i in enumerate(places):
+            pltpu.make_async_copy(stage.at[j], restored.at[i], stage_sem.at[j]).wait()
+
     copy.wait()
 
 
@@ -360,7 +377,8 @@
     _, slots, rows, width = saved.shape
     cols = width // m
     late = len(late_steps(n))
-    parts = parts_of(rows)
+    widths = parts_of(cols)
+    parts = len(widths)
     arrived, kept = pl.pallas_call(
         lambda *refs: exchange(n, m, *refs),
         out_shape=[
@@ -386,7 +404,7 @@
             pltpu.SemaphoreType.DMA,
             pltpu.SemaphoreType.DMA((2 * parts,)),
         ]
-        + [pltpu.VMEM((slots, rows // parts, cols), saved.dtype)] * parts,
+        + [pltpu.VMEM((slots, rows, width), saved.dtype) for width in widths],
         compiler_params=pltpu.CompilerParams(
             collective_id=0, has_side_effects=True, vmem_limit_bytes=20 * 2**20
         ),

time: 189 us -> 187 us (0.989); the launches traced: 189 us -> 183 us
  Pallas kernels: 188 us -> 182 us
    pallas_call x1, Pallas kernels: 17.4 us -> 0.11 us  [body(): pl.pallas_call(lambda *refs: exchange_late(n, m, *refs), out_shape=jax.Sh...]
    pallas_call x1, Pallas kernels: 163 us -> 176 us  [body(): pl.pallas_call(lambda *refs: exchange(n, m, *refs), out_shape=[jax.ShapeD...]
where the time goes in v3:
time: 187 us; the launch traced here: 183 us
  Pallas kernels  182 us (97%)
    pallas_call x1, Pallas kernels, body(): pl.pallas_call(lambda *refs: exchange(n, m, *refs), out_shape=[jax.ShapeD...  176 us
    pallas_call x1, Pallas kernels, body(): pl.pallas_call(lambda *refs: widen(n, *refs), out_shape=[jax.ShapeDtypeSt...  6.01 us

profile of v3, /device:TPU:8, one launch (start us, length us, event | category | flops | bytes accessed | tf_op | source)
XLA Modules:
  0.0 183.1 jit_solution(4446387935607164059)
XLA Ops:
  0.6 175.6 %exchange.1 = (bf16[16,64,4096]{2,1,0:T(8,128)(2,1)S(1)}, bf16[4,32,4096]{2,1,0:T(8,128)(2,1)S(1)}) custom-call(s32[1,16]{1,0:T(1,128)} %refs_0_.1, bf16[16,32,8192]{2,1,0:T(8,128)(2,1)} %bitcast.4), custom_call_target="tpu_custom_call" | custom-call | tf_op jit(solution)/shard_map/exchange/pallas_call | solution.py:382
  176.2 6.0 %widen.1 = (f32[16,64,4096]{2,1,0:T(8,128)}, f32[16,4096]{1,0:T(8,128)S(1)}) custom-call(bf16[16,64,4096]{2,1,0:T(8,128)(2,1)S(1)} %get-tuple-element.9.refs_0_), custom_call_target="tpu_custom_call" | custom-call | tf_op jit(solution)/shard_map/widen/pallas_call | solution.py:417
  182.2 0.1 exchange_late.1.refs_0_
  182.3 0.8 widen_late.1

commit v4 on v3

--- a/solution.py
+++ b/solution.py
@@ -293,8 +293,9 @@
             copy.wait()
 
 
-def widen_block(arrived, i, restored, sums, at, stage, sem, eager=False):
+def widen_block(arrived, i, restored, sums, at, stage, sem, row=None, eager=False):
     _, rows, cols = arrived.shape
+    row = at if row is None else row
     wide = min(cols, 512)
     for c in range(0, cols, wide):
         here = pl.ds(c, wide)
@@ -304,7 +305,7 @@
             part = arrived[i, band, here].astype(jnp.float32)
             stage[band, here] = part
             total = part if total is None else total + part
-        sums[pl.ds(at, 1), here] = jnp.sum(total, axis=0, keepdims=True)
+        sums[pl.ds(row, 1), here] = jnp.sum(total, axis=0, keepdims=True)
         if eager:
             pltpu.make_async_copy(stage.at[:, here], restored.at[at, :, here], sem).start()
     if eager:
@@ -348,19 +349,24 @@
         copy.wait()
 
 
-def widen_late(n, arrived, given, sums, restored, sums_out, stage, table, stage_sem, table_sem):
+def widen_late(n, arrived, given, sums, restored, sums_out, stage, fresh, table, stage_sem, table_sem):
     s = lax.axis_index("section")
     late = late_steps(n)
-    table[pl.ds(0, n), :] = sums[...]
-
     places = [partner(s, k, n) for k in late]
 
     @pl.when(is_late(s, n))
     def _():
         for j, i in enumerate(places):
             widen_block(
-                arrived, j, restored, table, i, stage.at[j], stage_sem.at[j], eager=True
+                arrived, j, restored, fresh, i, stage.at[j], stage_sem.at[j], row=j, eager=True
             )
+
+    table[pl.ds(0, n), :] = sums[...]
+
+    @pl.when(is_late(s, n))
+    def _():
+        for j, i in enumerate(places):
+            table[pl.ds(i, 1), :] = fresh[pl.ds(j, 1), :]
 
     copy = pltpu.make_async_copy(table.at[pl.ds(0, n), :], sums_out, table_sem)
     copy.start()
@@ -468,6 +474,7 @@
             ],
             scratch_shapes=[
                 pltpu.VMEM((late, height, cols), jnp.float32),
+                pltpu.VMEM((late + 8, cols), jnp.float32),
                 pltpu.VMEM((blocks + 8, cols), jnp.float32),
                 pltpu.SemaphoreType.DMA((late,)),
                 pltpu.SemaphoreType.DMA,

time: 187 us -> 187 us (level)
  no operation moved by 1% of the time
where the time goes in v4:
time: 187 us; the launch traced here: 183 us
  Pallas kernels  182 us (97%)
    pallas_call x1, Pallas kernels, body(): pl.pallas_call(lambda *refs: exchange(n, m, *refs), out_shape=[jax.ShapeD...  176 us
    pallas_call x1, Pallas kernels, body(): pl.pallas_call(lambda *refs: widen(n, *refs), out_shape=[jax.ShapeDtypeSt...  6.01 us

profile of v4, /device:TPU:8, one launch (start us, length us, event | category | flops | bytes accessed | tf_op | source)
XLA Modules:
  0.0 183.1 jit_solution(6134336477571771397)
XLA Ops:
  0.6 175.6 %exchange.1 = (bf16[16,64,4096]{2,1,0:T(8,128)(2,1)S(1)}, bf16[4,32,4096]{2,1,0:T(8,128)(2,1)S(1)}) custom-call(s32[1,16]{1,0:T(1,128)} %refs_0_.1, bf16[16,32,8192]{2,1,0:T(8,128)(2,1)} %bitcast.4), custom_call_target="tpu_custom_call" | custom-call | tf_op jit(solution)/shard_map/exchange/pallas_call | solution.py:388
  176.2 6.0 %widen.1 = (f32[16,64,4096]{2,1,0:T(8,128)}, f32[16,4096]{1,0:T(8,128)S(1)}) custom-call(bf16[16,64,4096]{2,1,0:T(8,128)(2,1)S(1)} %get-tuple-element.9.refs_0_), custom_call_target="tpu_custom_call" | custom-call | tf_op jit(solution)/shard_map/widen/pallas_call | solution.py:423
  182.2 0.1 exchange_late.1.refs_0_
  182.3 0.8 widen_late.1
